TPU v7x, 32 devices: a whole 2x2x4 slice. The times are simulated.
32 devices in a mesh: seq: 8 (over z, y), rep: 4 (over x, core).
Axes of the slice: x: 2, y: 2, z: 4, core: 2. Of those that a mesh axis runs over, the one named last changes fastest.
Arguments:
- head_out: bfloat16 [4, 4096, 4096], P('rep', 'seq'), may hold values from -6 to 6
- grad_out: bfloat16 [4, 4096, 3584], P('rep', 'seq'), may hold values from -6 to 6
- hash_codes: int32 [4, 16, 3584], P('rep'), may hold values from 0 to 511
- loss_mask: int32 [4096], P('seq'), may hold values 0 or 1
- query_ids: int32 [64], replicated, may hold values from 0 to 4095
Outputs:
- attribution: float32 [4096, 64], P(('seq', 'rep'))
All inputs are finite; a program needn't handle non-finite values. No bound on the sum of `loss_mask` on one device may be relied on, other than what follows from the above.
Results may differ from a plain program's by a relative error of at most 0.0025.
Values may be sent and summed in bfloat16 or wider, within the bound.
A program may use at most 64 MiB of HBM per device.

v0:
```python
import math
import jax
import jax.numpy as jnp
from jax import lax
from jax.sharding import PartitionSpec as P

ridge_shift = 0.25
norm_floor = 1e-06


def build_sketches(outputs, gradient, codes):
    head_count = codes.shape[0]
    sketch_width = outputs.shape[1] // head_count
    model_width = gradient.shape[1]
    sketch_scale = math.sqrt(sketch_width / model_width)
    columns = jnp.arange(sketch_width, dtype=jnp.int32)

    def one_head(head_index):
        head_codes = codes[head_index]
        bucket = head_codes % sketch_width
        sign_flip = 1 - 2 * (head_codes // sketch_width)
        count_table = jnp.where(bucket[:, None] == columns[None, :], sign_flip[:, None], 0).astype(
            jnp.bfloat16
        )
        counted = jnp.dot(gradient, count_table, preferred_element_type=jnp.float32)
        picked = lax.dynamic_slice_in_dim(
            outputs, head_index * sketch_width, sketch_width, 1
        ).astype(jnp.float32)
        return (picked * counted * sketch_scale).astype(jnp.bfloat16)

    return lax.map(one_head, jnp.arange(head_count, dtype=jnp.int32))


def solve_queries(gram_sum, chosen, token_count):
    sketch_width = gram_sum.shape[0]
    gram_sum = gram_sum / token_count + ridge_shift * jnp.eye(sketch_width, dtype=jnp.float32)
    factor = jnp.linalg.cholesky(gram_sum)
    return jax.scipy.linalg.cho_solve((factor, True), chosen.T).astype(jnp.bfloat16)


def on_device(head_out, grad_out, hash_codes, loss_mask, query_ids):
    sketches = build_sketches(head_out[0], grad_out[0], hash_codes[0])
    tok_rows = loss_mask.shape[0]
    out_rows = tok_rows // lax.axis_size("rep")
    mask_bf = loss_mask.astype(jnp.bfloat16)
    local_count = jnp.sum(loss_mask.astype(jnp.float32))
    token_count = lax.psum(local_count, "seq") + 1.0
    local_grams = jnp.einsum(
        "htk,htj->hkj",
        sketches * mask_bf[None, :, None],
        sketches,
        preferred_element_type=jnp.float32,
    )
    first_row = lax.axis_index("seq") * tok_rows
    query_hits = (
        query_ids[:, None] - first_row == jnp.arange(tok_rows, dtype=jnp.int32)[None, :]
    ).astype(jnp.bfloat16)
    local_chosen = jnp.einsum(
        "qt,htk->hqk", query_hits, sketches, preferred_element_type=jnp.float32
    )
    own_grams, own_chosen = (
        lax.psum_scatter(local_grams, "seq", scatter_dimension=0, tiled=True),
        lax.psum_scatter(local_chosen, "seq", scatter_dimension=0, tiled=True),
    )
    solved = jnp.stack(
        [
            solve_queries(own_grams[slot_index], own_chosen[slot_index], token_count)
            for slot_index in range(own_grams.shape[0])
        ]
    )
    solved_all = lax.all_gather(solved, "seq", axis=0, tiled=True)
    score_sum = jnp.einsum("htk,hkq->tq", sketches, solved_all, preferred_element_type=jnp.float32)
    contrib = lax.psum_scatter(score_sum, "rep", scatter_dimension=0, tiled=True)
    row_start = lax.axis_index("rep") * out_rows
    mask_rows = lax.dynamic_slice_in_dim(loss_mask, row_start, out_rows, 0).astype(jnp.float32)
    partial_value = jnp.sum(mask_rows[:, None] * contrib * contrib, 0)
    norm_sum = lax.psum(partial_value, ("seq", "rep")) / token_count
    return contrib / jnp.sqrt(norm_sum + norm_floor)


def solution(mesh):
    placed = (P("rep", "seq", None), P("rep", "seq", None), P("rep", None, None), P("seq"), P())
    return jax.shard_map(
        on_device, mesh=mesh, in_specs=placed, out_specs=P(("seq", "rep"), None), check_vma=False
    )
```

profile of v0, /device:TPU:0, one launch (start us, length us, event | category | flops | bytes accessed | tf_op | source)
XLA Modules:
  0.0 561.4 jit_solution(14292173351317738377)
XLA Ops:
  6.5 6.5 %copy.13 = bf16[1,512,4096]{1,2,0:T(8,128)(2,1)} copy(bf16[1,512,4096]{2,1,0:T(8,128)(2,1)} %param.10) | data formatting | bytes 8388608 | tf_op args[0]
  13.0 158.3 %while.17 = (s32[]{:T(128)}, bf16[16,512,256]{1,2,0:T(8,128)(2,1)}, s32[16]{0:T(128)S(1)}, bf16[512,4096]{0,1:T(8,128)(2,1)}, s32[16,3584]{1,0:T(8,128)}, /*inde...) while((s32[]{:T(128)}, bf16[16,512,256]{1,2,0:T(8,128)(2,1)}, ...), condition=%wide.region_1.2_spmd.clone, body=%wide.region_0.1_spmd.clone.sunk | while | flops 942876160 | bytes 4295377 | solution.py:31
  26.7 6.1 %fusion.76 = bf16[16,512,256]{1,2,0:T(8,128)(2,1)} fusion(bf16[16,512,256]{1,2,0:T(8,128)(2,1)} %get-tuple-element.293, s32[]{:T(128)} %get-tuple-element.292, bf16[512,3584]{1,0:T(8,128)(2,1)} %get-tuple-element.308, s32[3584]{0:T(1024)S(1)} %get-tuple-element.267, s32[3584]{0:T(1024)S(1)} %get-tuple-element.268, ...), kind=kOutput, calls=%fused_computation.16.clone.1 | convolution fusion | flops 942800896 | bytes 4223492 | tf_op jit(solution)/shard_map/while/body/eval_jaxpr/dot_general | solution.py:25
  36.6 6.1 %fusion.76 = bf16[16,512,256]{1,2,0:T(8,128)(2,1)} fusion(bf16[16,512,256]{1,2,0:T(8,128)(2,1)} %get-tuple-element.293, s32[]{:T(128)} %get-tuple-element.292, bf16[512,3584]{1,0:T(8,128)(2,1)} %get-tuple-element.308, s32[3584]{0:T(1024)S(1)} %get-tuple-element.267, s32[3584]{0:T(1024)S(1)} %get-tuple-element.268, ...), kind=kOutput, calls=%fused_computation.16.clone.1 | convolution fusion | flops 942800896 | bytes 4223492 | tf_op jit(solution)/shard_map/while/body/eval_jaxpr/dot_general | solution.py:25
  46.5 6.1 %fusion.76 = bf16[16,512,256]{1,2,0:T(8,128)(2,1)} fusion(bf16[16,512,256]{1,2,0:T(8,128)(2,1)} %get-tuple-element.293, s32[]{:T(128)} %get-tuple-element.292, bf16[512,3584]{1,0:T(8,128)(2,1)} %get-tuple-element.308, s32[3584]{0:T(1024)S(1)} %get-tuple-element.267, s32[3584]{0:T(1024)S(1)} %get-tuple-element.268, ...), kind=kOutput, calls=%fused_computation.16.clone.1 | convolution fusion | flops 942800896 | bytes 4223492 | tf_op jit(solution)/shard_map/while/body/eval_jaxpr/dot_general | solution.py:25
  56.4 6.1 %fusion.76 = bf16[16,512,256]{1,2,0:T(8,128)(2,1)} fusion(bf16[16,512,256]{1,2,0:T(8,128)(2,1)} %get-tuple-element.293, s32[]{:T(128)} %get-tuple-element.292, bf16[512,3584]{1,0:T(8,128)(2,1)} %get-tuple-element.308, s32[3584]{0:T(1024)S(1)} %get-tuple-element.267, s32[3584]{0:T(1024)S(1)} %get-tuple-element.268, ...), kind=kOutput, calls=%fused_computation.16.clone.1 | convolution fusion | flops 942800896 | bytes 4223492 | tf_op jit(solution)/shard_map/while/body/eval_jaxpr/dot_general | solution.py:25
  66.3 6.1 %fusion.76 = bf16[16,512,256]{1,2,0:T(8,128)(2,1)} fusion(bf16[16,512,256]{1,2,0:T(8,128)(2,1)} %get-tuple-element.293, s32[]{:T(128)} %get-tuple-element.292, bf16[512,3584]{1,0:T(8,128)(2,1)} %get-tuple-element.308, s32[3584]{0:T(1024)S(1)} %get-tuple-element.267, s32[3584]{0:T(1024)S(1)} %get-tuple-element.268, ...), kind=kOutput, calls=%fused_computation.16.clone.1 | convolution fusion | flops 942800896 | bytes 4223492 | tf_op jit(solution)/shard_map/while/body/eval_jaxpr/dot_general | solution.py:25
  76.2 6.1 %fusion.76 = bf16[16,512,256]{1,2,0:T(8,128)(2,1)} fusion(bf16[16,512,256]{1,2,0:T(8,128)(2,1)} %get-tuple-element.293, s32[]{:T(128)} %get-tuple-element.292, bf16[512,3584]{1,0:T(8,128)(2,1)} %get-tuple-element.308, s32[3584]{0:T(1024)S(1)} %get-tuple-element.267, s32[3584]{0:T(1024)S(1)} %get-tuple-element.268, ...), kind=kOutput, calls=%fused_computation.16.clone.1 | convolution fusion | flops 942800896 | bytes 4223492 | tf_op jit(solution)/shard_map/while/body/eval_jaxpr/dot_general | solution.py:25
  86.1 6.1 %fusion.76 = bf16[16,512,256]{1,2,0:T(8,128)(2,1)} fusion(bf16[16,512,256]{1,2,0:T(8,128)(2,1)} %get-tuple-element.293, s32[]{:T(128)} %get-tuple-element.292, bf16[512,3584]{1,0:T(8,128)(2,1)} %get-tuple-element.308, s32[3584]{0:T(1024)S(1)} %get-tuple-element.267, s32[3584]{0:T(1024)S(1)} %get-tuple-element.268, ...), kind=kOutput, calls=%fused_computation.16.clone.1 | convolution fusion | flops 942800896 | bytes 4223492 | tf_op jit(solution)/shard_map/while/body/eval_jaxpr/dot_general | solution.py:25
  96.0 6.1 %fusion.76 = bf16[16,512,256]{1,2,0:T(8,128)(2,1)} fusion(bf16[16,512,256]{1,2,0:T(8,128)(2,1)} %get-tuple-element.293, s32[]{:T(128)} %get-tuple-element.292, bf16[512,3584]{1,0:T(8,128)(2,1)} %get-tuple-element.308, s32[3584]{0:T(1024)S(1)} %get-tuple-element.267, s32[3584]{0:T(1024)S(1)} %get-tuple-element.268, ...), kind=kOutput, calls=%fused_computation.16.clone.1 | convolution fusion | flops 942800896 | bytes 4223492 | tf_op jit(solution)/shard_map/while/body/eval_jaxpr/dot_general | solution.py:25
  105.9 6.1 %fusion.76 = bf16[16,512,256]{1,2,0:T(8,128)(2,1)} fusion(bf16[16,512,256]{1,2,0:T(8,128)(2,1)} %get-tuple-element.293, s32[]{:T(128)} %get-tuple-element.292, bf16[512,3584]{1,0:T(8,128)(2,1)} %get-tuple-element.308, s32[3584]{0:T(1024)S(1)} %get-tuple-element.267, s32[3584]{0:T(1024)S(1)} %get-tuple-element.268, ...), kind=kOutput, calls=%fused_computation.16.clone.1 | convolution fusion | flops 942800896 | bytes 4223492 | tf_op jit(solution)/shard_map/while/body/eval_jaxpr/dot_general | solution.py:25
  115.7 6.1 %fusion.76 = bf16[16,512,256]{1,2,0:T(8,128)(2,1)} fusion(bf16[16,512,256]{1,2,0:T(8,128)(2,1)} %get-tuple-element.293, s32[]{:T(128)} %get-tuple-element.292, bf16[512,3584]{1,0:T(8,128)(2,1)} %get-tuple-element.308, s32[3584]{0:T(1024)S(1)} %get-tuple-element.267, s32[3584]{0:T(1024)S(1)} %get-tuple-element.268, ...), kind=kOutput, calls=%fused_computation.16.clone.1 | convolution fusion | flops 942800896 | bytes 4223492 | tf_op jit(solution)/shard_map/while/body/eval_jaxpr/dot_general | solution.py:25
  125.6 6.1 %fusion.76 = bf16[16,512,256]{1,2,0:T(8,128)(2,1)} fusion(bf16[16,512,256]{1,2,0:T(8,128)(2,1)} %get-tuple-element.293, s32[]{:T(128)} %get-tuple-element.292, bf16[512,3584]{1,0:T(8,128)(2,1)} %get-tuple-element.308, s32[3584]{0:T(1024)S(1)} %get-tuple-element.267, s32[3584]{0:T(1024)S(1)} %get-tuple-element.268, ...), kind=kOutput, calls=%fused_computation.16.clone.1 | convolution fusion | flops 942800896 | bytes 4223492 | tf_op jit(solution)/shard_map/while/body/eval_jaxpr/dot_general | solution.py:25
  135.6 6.1 %fusion.76 = bf16[16,512,256]{1,2,0:T(8,128)(2,1)} fusion(bf16[16,512,256]{1,2,0:T(8,128)(2,1)} %get-tuple-element.293, s32[]{:T(128)} %get-tuple-element.292, bf16[512,3584]{1,0:T(8,128)(2,1)} %get-tuple-element.308, s32[3584]{0:T(1024)S(1)} %get-tuple-element.267, s32[3584]{0:T(1024)S(1)} %get-tuple-element.268, ...), kind=kOutput, calls=%fused_computation.16.clone.1 | convolution fusion | flops 942800896 | bytes 4223492 | tf_op jit(solution)/shard_map/while/body/eval_jaxpr/dot_general | solution.py:25
  145.4 6.1 %fusion.76 = bf16[16,512,256]{1,2,0:T(8,128)(2,1)} fusion(bf16[16,512,256]{1,2,0:T(8,128)(2,1)} %get-tuple-element.293, s32[]{:T(128)} %get-tuple-element.292, bf16[512,3584]{1,0:T(8,128)(2,1)} %get-tuple-element.308, s32[3584]{0:T(1024)S(1)} %get-tuple-element.267, s32[3584]{0:T(1024)S(1)} %get-tuple-element.268, ...), kind=kOutput, calls=%fused_computation.16.clone.1 | convolution fusion | flops 942800896 | bytes 4223492 | tf_op jit(solution)/shard_map/while/body/eval_jaxpr/dot_general | solution.py:25
  155.3 6.1 %fusion.76 = bf16[16,512,256]{1,2,0:T(8,128)(2,1)} fusion(bf16[16,512,256]{1,2,0:T(8,128)(2,1)} %get-tuple-element.293, s32[]{:T(128)} %get-tuple-element.292, bf16[512,3584]{1,0:T(8,128)(2,1)} %get-tuple-element.308, s32[3584]{0:T(1024)S(1)} %get-tuple-element.267, s32[3584]{0:T(1024)S(1)} %get-tuple-element.268, ...), kind=kOutput, calls=%fused_computation.16.clone.1 | convolution fusion | flops 942800896 | bytes 4223492 | tf_op jit(solution)/shard_map/while/body/eval_jaxpr/dot_general | solution.py:25
  165.2 6.1 %fusion.76 = bf16[16,512,256]{1,2,0:T(8,128)(2,1)} fusion(bf16[16,512,256]{1,2,0:T(8,128)(2,1)} %get-tuple-element.293, s32[]{:T(128)} %get-tuple-element.292, bf16[512,3584]{1,0:T(8,128)(2,1)} %get-tuple-element.308, s32[3584]{0:T(1024)S(1)} %get-tuple-element.267, s32[3584]{0:T(1024)S(1)} %get-tuple-element.268, ...), kind=kOutput, calls=%fused_computation.16.clone.1 | convolution fusion | flops 942800896 | bytes 4223492 | tf_op jit(solution)/shard_map/while/body/eval_jaxpr/dot_general | solution.py:25
  176.0 6.7 %fusion.17 = f32[16,256,256]{1,2,0:T(8,128)} fusion(bf16[16,512,256]{1,2,0:T(8,128)(2,1)} %get-tuple-element.99, bf16[512]{0:T(512)(128)(2,1)S(1)} %convert_element_type.36), kind=kOutput, calls=%fused_computation.29 | convolution fusion | flops 1075838976 | bytes 8389632 | tf_op jit(solution)/shard_map/htk,htj->hkj/dot_general | solution.py:48
  183.4 24.0 %psum.14 = f32[]{:T(128)} all-reduce(f32[]{:T(128)} %convert_reduce_fusion), channel_id=1, replica_groups=mesh['seq'=8,'rep'=4] {'seq'}, use_global_device_ids=true, to_apply=%region_4.5 | all-reduce | flops 1 | bytes 8 | tf_op jit(solution)/shard_map/psum | solution.py:47
  208.0 34.9 %reduce-scatter.6.cloned.1.call-done = f32[2,64,256]{2,1,0:T(8,128)} async-done(((f32[16,64,256]{2,1,0:T(8,128)}), f32[2,64,256]{2,1,0:T(8,128)}) %reduce-scatter.6.cloned.1.call-update) | async-done | bytes 131088 | tf_op jit(solution)/shard_map/reduce_scatter | solution.py:63
  243.8 90.0 %reduce-scatter.4.cloned.1.call-done = f32[2,256,256]{1,2,0:T(8,128)} async-done(((f32[16,256,256]{1,2,0:T(8,128)}), f32[2,256,256]{1,2,0:T(8,128)}) %reduce-scatter.4.cloned.1.call-update) | async-done | bytes 524304 | tf_op jit(solution)/shard_map/reduce_scatter | solution.py:62
  335.3 11.7 %cholesky.130 = f32[128,128]{1,0:T(8,128)S(1)} custom-call(f32[128,128]{1,0:T(8,128)S(1)} %cholesky.194), custom_call_target="Cholesky" | custom-call | tf_op jit(solution)/shard_map/jit(cholesky)/cholesky | solution.py:37
  347.0 9.8 %custom-call.15 = f32[1,128,128]{1,2,0:T(8,128)S(1)} custom-call(f32[1,128,128]{2,1,0:T(8,128)S(1)} %get-tuple-element.171), custom_call_target="InvertDiagBlocksLowerTriangular" | custom-call | tf_op jit(solution)/shard_map/jit(cholesky)/cholesky | solution.py:37
  357.3 11.7 %cholesky.147 = f32[128,128]{1,0:T(8,128)S(1)} custom-call(f32[128,128]{1,0:T(8,128)S(1)} %convolution_subtract_fusion.1), custom_call_target="Cholesky" | custom-call | tf_op jit(solution)/shard_map/jit(cholesky)/cholesky | solution.py:37
  375.4 19.9 %custom-call.16 = f32[2,128,128]{1,2,0:T(8,128)S(1)} custom-call(f32[2,128,128]{2,1,0:T(8,128)S(1)} %get-tuple-element.128), custom_call_target="InvertDiagBlocksLowerTriangular" | custom-call | tf_op jit(solution)/shard_map/jit(_cho_solve)/triangular_solve | solution.py:38
  396.8 11.7 %cholesky.164 = f32[128,128]{1,0:T(8,128)S(1)} custom-call(f32[128,128]{1,0:T(8,128)S(1)} %cholesky.197), custom_call_target="Cholesky" | custom-call | tf_op jit(solution)/shard_map/jit(cholesky)/cholesky | solution.py:37
  408.6 9.8 %custom-call.17 = f32[1,128,128]{1,2,0:T(8,128)S(1)} custom-call(f32[1,128,128]{2,1,0:T(8,128)S(1)} %get-tuple-element.175), custom_call_target="InvertDiagBlocksLowerTriangular" | custom-call | tf_op jit(solution)/shard_map/jit(cholesky)/cholesky | solution.py:37
  418.9 11.7 %cholesky.181 = f32[128,128]{1,0:T(8,128)S(1)} custom-call(f32[128,128]{1,0:T(8,128)S(1)} %convolution_subtract_fusion), custom_call_target="Cholesky" | custom-call | tf_op jit(solution)/shard_map/jit(cholesky)/cholesky | solution.py:37
  437.4 19.9 %custom-call.18 = f32[2,128,128]{1,2,0:T(8,128)S(1)} custom-call(f32[2,128,128]{2,1,0:T(8,128)S(1)} %get-tuple-element.129), custom_call_target="InvertDiagBlocksLowerTriangular" | custom-call | tf_op jit(solution)/shard_map/jit(_cho_solve)/triangular_solve | solution.py:38
  458.8 31.4 %all_gather.3 = bf16[16,256,64]{1,2,0:T(8,128)(2,1)S(1)} all-gather(bf16[2,256,64]{1,2,0:T(8,128)(2,1)S(1)} %pad_maximum_fusion), channel_id=1, replica_groups=mesh['seq'=8,'rep'=4] {'seq'}, dimensions={0}, use_global_device_ids=true | all-gather | bytes 589824 | tf_op jit(solution)/shard_map/all_gather | solution.py:71
  494.0 19.3 %reduce-scatter.8.cloned.1.call-done = f32[128,64]{0,1:T(8,128)} async-done(((f32[512,64]{0,1:T(8,128)}), f32[128,64]{0,1:T(8,128)}) %reduce-scatter.8.cloned.1.call-update) | async-done | bytes 32784 | tf_op jit(solution)/shard_map/reduce_scatter | solution.py:73
  514.1 39.3 %psum.15 = f32[64]{0:T(128)S(1)} all-reduce(f32[64]{0:T(128)S(1)} %fusion.45), channel_id=1, replica_groups=mesh['seq'=8,'rep'=4] {'seq','rep'}, use_global_device_ids=true, to_apply=%region_12.15 | all-reduce | flops 64 | bytes 512 | tf_op jit(solution)/shard_map/psum | solution.py:77
  (126 shorter events, 66.5 us)
Async XLA Ops:
  6.5 236.4 %reduce-scatter.6.cloned.1.call-start = ((), (), s32[]{:S(2)}) async-start(), calls=%async_computation.4 | async-start | bytes 1179648 | tf_op jit(solution)/shard_map/reduce_scatter | solution.py:63
  13.0 158.3 %copy-start.1 = (s32[64]{0:T(128)S(1)}, s32[64]{0:T(128)}, u32[]{:S(2)}) copy-start(s32[64]{0:T(128)} %param.14) | copy-start | bytes 772
  171.3 4.7 copy-start
  176.0 157.9 %reduce-scatter.4.cloned.1.call-start = ((), (), s32[]{:S(2)}) async-start(), calls=%async_computation.3 | async-start | bytes 4718592 | tf_op jit(solution)/shard_map/reduce_scatter | solution.py:62
  182.8 330.5 %reduce-scatter.8.cloned.1.call-start = ((), (), s32[]{:S(2)}) async-start(), calls=%async_computation.5 | async-start | bytes 163840 | tf_op jit(solution)/shard_map/reduce_scatter | solution.py:73
Sparse Core Ops, SparseCore 0:
  176.1 66.8 reduce-scatter.5
  246.6 87.2 reduce-scatter.3
  494.0 19.2 reduce-scatter.7
where the time goes:
time: 564 us; the launch traced here: 561 us
  waiting for transfers between devices  144 us (26%)
  matrix products  116 us (21%)
  other arithmetic  114 us (20%)
  blocking collectives  94.6 us (17%)
  local copies, waits for them, and re-layouts  39.5 us (7%)
  loops' own time  36.8 us (7%)
  between operations  16.5 us (3%)
    dot_general x16, matrix products, one_head(): counted = jnp.dot(gradient, count_table, preferred_element_type=jnp.float32)  97.2 us
    reduce_scatter x1, waiting for transfers between devices, on_device(): lax.psum_scatter(local_grams, 'seq', scatter_dimension=0, tiled=True)  90 us
    another operation x14, other arithmetic, solve_queries(): factor = jnp.linalg.cholesky(gram_sum)  69.2 us
    another operation x5, other arithmetic, solve_queries(): jax.scipy.linalg.cho_solve((factor, True), chosen.T).astype(jnp.bfloat16)  39.9 us
    psum x1, blocking collectives, on_device(): norm_sum = lax.psum(partial_value, ('seq', 'rep')) / token_count  39.3 us
    another operation x1, loops' own time, build_sketches(): return lax.map(one_head, jnp.arange(head_count, dtype=jnp.int32))  36.7 us
    reduce_scatter x1, waiting for transfers between devices, on_device(): lax.psum_scatter(local_chosen, 'seq', scatter_dimension=0, tiled=True)  34.9 us
    all_gather x1, blocking collectives, on_device(): solved_all = lax.all_gather(solved, 'seq', axis=0, tiled=True)  31.4 us
  transfers between devices with their start and end apart: 3, of which 3 were waited for; matrix products, arithmetic and copies ran while one was open for 1% of the time, Pallas kernels for 0%

commit v1 on v0

--- a/solution.py
+++ b/solution.py
@@ -6,6 +6,12 @@
 
 ridge_shift = 0.25
 norm_floor = 1e-06
+
+
+def gather_and_add(value, mesh_axis):
+    blocks = lax.all_gather(value, mesh_axis, axis=0, tiled=False)
+    summed = blocks.sum(axis=0)
+    return summed
 
 
 def build_sketches(outputs, gradient, codes):
@@ -74,7 +80,7 @@
     row_start = lax.axis_index("rep") * out_rows
     mask_rows = lax.dynamic_slice_in_dim(loss_mask, row_start, out_rows, 0).astype(jnp.float32)
     partial_value = jnp.sum(mask_rows[:, None] * contrib * contrib, 0)
-    norm_sum = lax.psum(partial_value, ("seq", "rep")) / token_count
+    norm_sum = gather_and_add(partial_value, ("seq", "rep")) / token_count
     return contrib / jnp.sqrt(norm_sum + norm_floor)
 
 

time: 564 us -> 564 us (level)
    unnamed x0 -> x1, blocking collectives: none -> 39.3 us
    psum x1 -> x0, blocking collectives: 39.3 us -> none  [on_device(): norm_sum = lax.psum(partial_value, ('seq', 'rep')) / token_count]
where the time goes in v1:
time: 564 us; the launch traced here: 562 us
  waiting for transfers between devices  144 us (26%)
  matrix products  116 us (21%)
  other arithmetic  114 us (20%)
  blocking collectives  94.6 us (17%)
  local copies, waits for them, and re-layouts  39.9 us (7%)
  loops' own time  36.8 us (7%)
  between operations  16.5 us (3%)
    dot_general x16, matrix products, one_head(): counted = jnp.dot(gradient, count_table, preferred_element_type=jnp.float32)  97.2 us
    reduce_scatter x1, waiting for transfers between devices, on_device(): lax.psum_scatter(local_grams, 'seq', scatter_dimension=0, tiled=True)  90 us
    another operation x14, other arithmetic, solve_queries(): factor = jnp.linalg.cholesky(gram_sum)  69.2 us
    another operation x5, other arithmetic, solve_queries(): jax.scipy.linalg.cho_solve((factor, True), chosen.T).astype(jnp.bfloat16)  39.9 us
    unnamed x1, blocking collectives  39.3 us
    another operation x1, loops' own time, build_sketches(): return lax.map(one_head, jnp.arange(head_count, dtype=jnp.int32))  36.7 us
    reduce_scatter x1, waiting for transfers between devices, on_device(): lax.psum_scatter(local_chosen, 'seq', scatter_dimension=0, tiled=True)  34.9 us
    all_gather x1, blocking collectives, on_device(): solved_all = lax.all_gather(solved, 'seq', axis=0, tiled=True)  31.4 us
  transfers between devices with their start and end apart: 3, of which 3 were waited for; matrix products, arithmetic and copies ran while one was open for 1% of the time, Pallas kernels for 0%

profile of v1, /device:TPU:0, one launch (start us, length us, event | category | flops | bytes accessed | tf_op | source)
XLA Modules:
  0.0 561.5 jit_solution(14013833207641903197)
XLA Ops:
  6.5 6.5 %copy.20 = bf16[1,512,4096]{1,2,0:T(8,128)(2,1)} copy(bf16[1,512,4096]{2,1,0:T(8,128)(2,1)} %param.10) | data formatting | bytes 8388608 | tf_op args[0]
  13.0 158.3 %while.17 = (s32[]{:T(128)}, bf16[16,512,256]{1,2,0:T(8,128)(2,1)}, s32[16]{0:T(128)S(1)}, bf16[512,4096]{0,1:T(8,128)(2,1)}, s32[16,3584]{1,0:T(8,128)}, /*inde...) while((s32[]{:T(128)}, bf16[16,512,256]{1,2,0:T(8,128)(2,1)}, ...), condition=%wide.region_1.2_spmd.clone, body=%wide.region_0.1_spmd.clone.sunk | while | flops 942876160 | bytes 4295377 | solution.py:37
  26.7 6.1 %fusion.76 = bf16[16,512,256]{1,2,0:T(8,128)(2,1)} fusion(bf16[16,512,256]{1,2,0:T(8,128)(2,1)} %get-tuple-element.293, s32[]{:T(128)} %get-tuple-element.292, bf16[512,3584]{1,0:T(8,128)(2,1)} %get-tuple-element.308, s32[3584]{0:T(1024)S(1)} %get-tuple-element.267, s32[3584]{0:T(1024)S(1)} %get-tuple-element.268, ...), kind=kOutput, calls=%fused_computation.16.clone.1 | convolution fusion | flops 942800896 | bytes 4223492 | tf_op jit(solution)/shard_map/while/body/eval_jaxpr/dot_general | solution.py:31
  36.6 6.1 %fusion.76 = bf16[16,512,256]{1,2,0:T(8,128)(2,1)} fusion(bf16[16,512,256]{1,2,0:T(8,128)(2,1)} %get-tuple-element.293, s32[]{:T(128)} %get-tuple-element.292, bf16[512,3584]{1,0:T(8,128)(2,1)} %get-tuple-element.308, s32[3584]{0:T(1024)S(1)} %get-tuple-element.267, s32[3584]{0:T(1024)S(1)} %get-tuple-element.268, ...), kind=kOutput, calls=%fused_computation.16.clone.1 | convolution fusion | flops 942800896 | bytes 4223492 | tf_op jit(solution)/shard_map/while/body/eval_jaxpr/dot_general | solution.py:31
  46.5 6.1 %fusion.76 = bf16[16,512,256]{1,2,0:T(8,128)(2,1)} fusion(bf16[16,512,256]{1,2,0:T(8,128)(2,1)} %get-tuple-element.293, s32[]{:T(128)} %get-tuple-element.292, bf16[512,3584]{1,0:T(8,128)(2,1)} %get-tuple-element.308, s32[3584]{0:T(1024)S(1)} %get-tuple-element.267, s32[3584]{0:T(1024)S(1)} %get-tuple-element.268, ...), kind=kOutput, calls=%fused_computation.16.clone.1 | convolution fusion | flops 942800896 | bytes 4223492 | tf_op jit(solution)/shard_map/while/body/eval_jaxpr/dot_general | solution.py:31
  56.4 6.1 %fusion.76 = bf16[16,512,256]{1,2,0:T(8,128)(2,1)} fusion(bf16[16,512,256]{1,2,0:T(8,128)(2,1)} %get-tuple-element.293, s32[]{:T(128)} %get-tuple-element.292, bf16[512,3584]{1,0:T(8,128)(2,1)} %get-tuple-element.308, s32[3584]{0:T(1024)S(1)} %get-tuple-element.267, s32[3584]{0:T(1024)S(1)} %get-tuple-element.268, ...), kind=kOutput, calls=%fused_computation.16.clone.1 | convolution fusion | flops 942800896 | bytes 4223492 | tf_op jit(solution)/shard_map/while/body/eval_jaxpr/dot_general | solution.py:31
  66.3 6.1 %fusion.76 = bf16[16,512,256]{1,2,0:T(8,128)(2,1)} fusion(bf16[16,512,256]{1,2,0:T(8,128)(2,1)} %get-tuple-element.293, s32[]{:T(128)} %get-tuple-element.292, bf16[512,3584]{1,0:T(8,128)(2,1)} %get-tuple-element.308, s32[3584]{0:T(1024)S(1)} %get-tuple-element.267, s32[3584]{0:T(1024)S(1)} %get-tuple-element.268, ...), kind=kOutput, calls=%fused_computation.16.clone.1 | convolution fusion | flops 942800896 | bytes 4223492 | tf_op jit(solution)/shard_map/while/body/eval_jaxpr/dot_general | solution.py:31
  76.2 6.1 %fusion.76 = bf16[16,512,256]{1,2,0:T(8,128)(2,1)} fusion(bf16[16,512,256]{1,2,0:T(8,128)(2,1)} %get-tuple-element.293, s32[]{:T(128)} %get-tuple-element.292, bf16[512,3584]{1,0:T(8,128)(2,1)} %get-tuple-element.308, s32[3584]{0:T(1024)S(1)} %get-tuple-element.267, s32[3584]{0:T(1024)S(1)} %get-tuple-element.268, ...), kind=kOutput, calls=%fused_computation.16.clone.1 | convolution fusion | flops 942800896 | bytes 4223492 | tf_op jit(solution)/shard_map/while/body/eval_jaxpr/dot_general | solution.py:31
  86.1 6.1 %fusion.76 = bf16[16,512,256]{1,2,0:T(8,128)(2,1)} fusion(bf16[16,512,256]{1,2,0:T(8,128)(2,1)} %get-tuple-element.293, s32[]{:T(128)} %get-tuple-element.292, bf16[512,3584]{1,0:T(8,128)(2,1)} %get-tuple-element.308, s32[3584]{0:T(1024)S(1)} %get-tuple-element.267, s32[3584]{0:T(1024)S(1)} %get-tuple-element.268, ...), kind=kOutput, calls=%fused_computation.16.clone.1 | convolution fusion | flops 942800896 | bytes 4223492 | tf_op jit(solution)/shard_map/while/body/eval_jaxpr/dot_general | solution.py:31
  96.0 6.1 %fusion.76 = bf16[16,512,256]{1,2,0:T(8,128)(2,1)} fusion(bf16[16,512,256]{1,2,0:T(8,128)(2,1)} %get-tuple-element.293, s32[]{:T(128)} %get-tuple-element.292, bf16[512,3584]{1,0:T(8,128)(2,1)} %get-tuple-element.308, s32[3584]{0:T(1024)S(1)} %get-tuple-element.267, s32[3584]{0:T(1024)S(1)} %get-tuple-element.268, ...), kind=kOutput, calls=%fused_computation.16.clone.1 | convolution fusion | flops 942800896 | bytes 4223492 | tf_op jit(solution)/shard_map/while/body/eval_jaxpr/dot_general | solution.py:31
  105.9 6.1 %fusion.76 = bf16[16,512,256]{1,2,0:T(8,128)(2,1)} fusion(bf16[16,512,256]{1,2,0:T(8,128)(2,1)} %get-tuple-element.293, s32[]{:T(128)} %get-tuple-element.292, bf16[512,3584]{1,0:T(8,128)(2,1)} %get-tuple-element.308, s32[3584]{0:T(1024)S(1)} %get-tuple-element.267, s32[3584]{0:T(1024)S(1)} %get-tuple-element.268, ...), kind=kOutput, calls=%fused_computation.16.clone.1 | convolution fusion | flops 942800896 | bytes 4223492 | tf_op jit(solution)/shard_map/while/body/eval_jaxpr/dot_general | solution.py:31
  115.7 6.1 %fusion.76 = bf16[16,512,256]{1,2,0:T(8,128)(2,1)} fusion(bf16[16,512,256]{1,2,0:T(8,128)(2,1)} %get-tuple-element.293, s32[]{:T(128)} %get-tuple-element.292, bf16[512,3584]{1,0:T(8,128)(2,1)} %get-tuple-element.308, s32[3584]{0:T(1024)S(1)} %get-tuple-element.267, s32[3584]{0:T(1024)S(1)} %get-tuple-element.268, ...), kind=kOutput, calls=%fused_computation.16.clone.1 | convolution fusion | flops 942800896 | bytes 4223492 | tf_op jit(solution)/shard_map/while/body/eval_jaxpr/dot_general | solution.py:31
  125.6 6.1 %fusion.76 = bf16[16,512,256]{1,2,0:T(8,128)(2,1)} fusion(bf16[16,512,256]{1,2,0:T(8,128)(2,1)} %get-tuple-element.293, s32[]{:T(128)} %get-tuple-element.292, bf16[512,3584]{1,0:T(8,128)(2,1)} %get-tuple-element.308, s32[3584]{0:T(1024)S(1)} %get-tuple-element.267, s32[3584]{0:T(1024)S(1)} %get-tuple-element.268, ...), kind=kOutput, calls=%fused_computation.16.clone.1 | convolution fusion | flops 942800896 | bytes 4223492 | tf_op jit(solution)/shard_map/while/body/eval_jaxpr/dot_general | solution.py:31
  135.6 6.1 %fusion.76 = bf16[16,512,256]{1,2,0:T(8,128)(2,1)} fusion(bf16[16,512,256]{1,2,0:T(8,128)(2,1)} %get-tuple-element.293, s32[]{:T(128)} %get-tuple-element.292, bf16[512,3584]{1,0:T(8,128)(2,1)} %get-tuple-element.308, s32[3584]{0:T(1024)S(1)} %get-tuple-element.267, s32[3584]{0:T(1024)S(1)} %get-tuple-element.268, ...), kind=kOutput, calls=%fused_computation.16.clone.1 | convolution fusion | flops 942800896 | bytes 4223492 | tf_op jit(solution)/shard_map/while/body/eval_jaxpr/dot_general | solution.py:31
  145.4 6.1 %fusion.76 = bf16[16,512,256]{1,2,0:T(8,128)(2,1)} fusion(bf16[16,512,256]{1,2,0:T(8,128)(2,1)} %get-tuple-element.293, s32[]{:T(128)} %get-tuple-element.292, bf16[512,3584]{1,0:T(8,128)(2,1)} %get-tuple-element.308, s32[3584]{0:T(1024)S(1)} %get-tuple-element.267, s32[3584]{0:T(1024)S(1)} %get-tuple-element.268, ...), kind=kOutput, calls=%fused_computation.16.clone.1 | convolution fusion | flops 942800896 | bytes 4223492 | tf_op jit(solution)/shard_map/while/body/eval_jaxpr/dot_general | solution.py:31
  155.3 6.1 %fusion.76 = bf16[16,512,256]{1,2,0:T(8,128)(2,1)} fusion(bf16[16,512,256]{1,2,0:T(8,128)(2,1)} %get-tuple-element.293, s32[]{:T(128)} %get-tuple-element.292, bf16[512,3584]{1,0:T(8,128)(2,1)} %get-tuple-element.308, s32[3584]{0:T(1024)S(1)} %get-tuple-element.267, s32[3584]{0:T(1024)S(1)} %get-tuple-element.268, ...), kind=kOutput, calls=%fused_computation.16.clone.1 | convolution fusion | flops 942800896 | bytes 4223492 | tf_op jit(solution)/shard_map/while/body/eval_jaxpr/dot_general | solution.py:31
  165.2 6.1 %fusion.76 = bf16[16,512,256]{1,2,0:T(8,128)(2,1)} fusion(bf16[16,512,256]{1,2,0:T(8,128)(2,1)} %get-tuple-element.293, s32[]{:T(128)} %get-tuple-element.292, bf16[512,3584]{1,0:T(8,128)(2,1)} %get-tuple-element.308, s32[3584]{0:T(1024)S(1)} %get-tuple-element.267, s32[3584]{0:T(1024)S(1)} %get-tuple-element.268, ...), kind=kOutput, calls=%fused_computation.16.clone.1 | convolution fusion | flops 942800896 | bytes 4223492 | tf_op jit(solution)/shard_map/while/body/eval_jaxpr/dot_general | solution.py:31
  176.0 6.7 %fusion.17 = f32[16,256,256]{1,2,0:T(8,128)} fusion(bf16[16,512,256]{1,2,0:T(8,128)(2,1)} %get-tuple-element.99, bf16[512]{0:T(512)(128)(2,1)S(1)} %convert_element_type.36), kind=kOutput, calls=%fused_computation.29 | convolution fusion | flops 1075838976 | bytes 8389632 | tf_op jit(solution)/shard_map/htk,htj->hkj/dot_general | solution.py:54
  183.4 24.0 %psum.7 = f32[]{:T(128)} all-reduce(f32[]{:T(128)} %convert_reduce_fusion), channel_id=1, replica_groups=mesh['seq'=8,'rep'=4] {'seq'}, use_global_device_ids=true, to_apply=%region_4.5 | all-reduce | flops 1 | bytes 8 | tf_op jit(solution)/shard_map/psum | solution.py:53
  208.0 34.9 %reduce-scatter.6.cloned.1.call-done = f32[2,64,256]{2,1,0:T(8,128)} async-done(((f32[16,64,256]{2,1,0:T(8,128)}), f32[2,64,256]{2,1,0:T(8,128)}) %reduce-scatter.6.cloned.1.call-update) | async-done | bytes 131088 | tf_op jit(solution)/shard_map/reduce_scatter | solution.py:69
  243.8 90.0 %reduce-scatter.4.cloned.1.call-done = f32[2,256,256]{1,2,0:T(8,128)} async-done(((f32[16,256,256]{1,2,0:T(8,128)}), f32[2,256,256]{1,2,0:T(8,128)}) %reduce-scatter.4.cloned.1.call-update) | async-done | bytes 524304 | tf_op jit(solution)/shard_map/reduce_scatter | solution.py:68
  335.3 11.7 %cholesky.130 = f32[128,128]{1,0:T(8,128)S(1)} custom-call(f32[128,128]{1,0:T(8,128)S(1)} %cholesky.194), custom_call_target="Cholesky" | custom-call | tf_op jit(solution)/shard_map/jit(cholesky)/cholesky | solution.py:43
  347.0 9.8 %custom-call.15 = f32[1,128,128]{1,2,0:T(8,128)S(1)} custom-call(f32[1,128,128]{2,1,0:T(8,128)S(1)} %get-tuple-element.171), custom_call_target="InvertDiagBlocksLowerTriangular" | custom-call | tf_op jit(solution)/shard_map/jit(cholesky)/cholesky | solution.py:43
  357.3 11.7 %cholesky.147 = f32[128,128]{1,0:T(8,128)S(1)} custom-call(f32[128,128]{1,0:T(8,128)S(1)} %convolution_subtract_fusion.1), custom_call_target="Cholesky" | custom-call | tf_op jit(solution)/shard_map/jit(cholesky)/cholesky | solution.py:43
  375.4 19.9 %custom-call.16 = f32[2,128,128]{1,2,0:T(8,128)S(1)} custom-call(f32[2,128,128]{2,1,0:T(8,128)S(1)} %get-tuple-element.128), custom_call_target="InvertDiagBlocksLowerTriangular" | custom-call | tf_op jit(solution)/shard_map/jit(_cho_solve)/triangular_solve | solution.py:44
  396.7 11.7 %cholesky.164 = f32[128,128]{1,0:T(8,128)S(1)} custom-call(f32[128,128]{1,0:T(8,128)S(1)} %cholesky.197), custom_call_target="Cholesky" | custom-call | tf_op jit(solution)/shard_map/jit(cholesky)/cholesky | solution.py:43
  408.4 9.8 %custom-call.17 = f32[1,128,128]{1,2,0:T(8,128)S(1)} custom-call(f32[1,128,128]{2,1,0:T(8,128)S(1)} %get-tuple-element.175), custom_call_target="InvertDiagBlocksLowerTriangular" | custom-call | tf_op jit(solution)/shard_map/jit(cholesky)/cholesky | solution.py:43
  418.8 11.7 %cholesky.181 = f32[128,128]{1,0:T(8,128)S(1)} custom-call(f32[128,128]{1,0:T(8,128)S(1)} %convolution_subtract_fusion), custom_call_target="Cholesky" | custom-call | tf_op jit(solution)/shard_map/jit(cholesky)/cholesky | solution.py:43
  437.3 19.9 %custom-call.18 = f32[2,128,128]{1,2,0:T(8,128)S(1)} custom-call(f32[2,128,128]{2,1,0:T(8,128)S(1)} %get-tuple-element.129), custom_call_target="InvertDiagBlocksLowerTriangular" | custom-call | tf_op jit(solution)/shard_map/jit(_cho_solve)/triangular_solve | solution.py:44
  458.5 31.4 %all_gather.9 = bf16[16,256,64]{1,2,0:T(8,128)(2,1)S(1)} all-gather(bf16[2,256,64]{1,2,0:T(8,128)(2,1)S(1)} %pad_maximum_fusion), channel_id=1, replica_groups=mesh['seq'=8,'rep'=4] {'seq'}, dimensions={0}, use_global_device_ids=true | all-gather | bytes 589824 | tf_op jit(solution)/shard_map/all_gather | solution.py:77
  493.7 19.3 %reduce-scatter.8.cloned.1.call-done = f32[128,64]{0,1:T(8,128)} async-done(((f32[512,64]{0,1:T(8,128)}), f32[128,64]{0,1:T(8,128)}) %reduce-scatter.8.cloned.1.call-update) | async-done | bytes 32784 | tf_op jit(solution)/shard_map/reduce_scatter | solution.py:79
  514.1 39.3 %all-reduce.1 = f32[2048]{0:T(1024)S(1)} all-reduce(f32[2048]{0:T(1024)S(1)} %dynamic-update-slice.9), channel_id=2, replica_groups=mesh['seq'=8,'rep'=4] {'seq','rep'}, use_global_device_ids=true, to_apply=%add.1 | all-reduce | flops 2048 | bytes 16384
  (130 shorter events, 66.6 us)
Async XLA Ops:
  6.5 236.4 %reduce-scatter.6.cloned.1.call-start = ((), (), s32[]{:S(2)}) async-start(), calls=%async_computation.4 | async-start | bytes 1179648 | tf_op jit(solution)/shard_map/reduce_scatter | solution.py:69
  13.0 158.3 %copy-start.1 = (s32[64]{0:T(128)S(1)}, s32[64]{0:T(128)}, u32[]{:S(2)}) copy-start(s32[64]{0:T(128)} %param.14) | copy-start | bytes 772
  171.3 4.7 copy-start
  176.0 157.9 %reduce-scatter.4.cloned.1.call-start = ((), (), s32[]{:S(2)}) async-start(), calls=%async_computation.3 | async-start | bytes 4718592 | tf_op jit(solution)/shard_map/reduce_scatter | solution.py:68
  182.8 330.2 %reduce-scatter.8.cloned.1.call-start = ((), (), s32[]{:S(2)}) async-start(), calls=%async_computation.5 | async-start | bytes 163840 | tf_op jit(solution)/shard_map/reduce_scatter | solution.py:79
Sparse Core Ops, SparseCore 0:
  176.1 66.8 reduce-scatter.5
  246.6 87.2 reduce-scatter.3
  493.7 19.1 reduce-scatter.7
